TPU v7x, 512 devices: a whole 4x4x16 slice. The times are simulated.
512 devices in a mesh: slab: 128 (over z_lo, y, x, core), det: 4 (over z_hi).
Axes of the slice: x: 4, y: 4, z: 16 (z_hi: 4, z_lo: 4; z = z_hi * 4 + z_lo), core: 2. Of those that a mesh axis runs over, the one named last changes fastest.
Arguments:
- traces: float32 [512, 128, 4096], P(('slab', 'det')), may hold values from -6 to 6
- tables: bfloat16 [512, 256, 2048], P('slab', None, 'det'), may hold values from -0.0625 to 0.0625
- slab_range: int32 [512, 2], P(('slab', 'det')), may hold values from 0 to 127, as said below
- table_slot: int32 [512, 7], P(('slab', 'det')), may hold values from 0 to 3
- sample_start: int32 [512, 7], P(('slab', 'det')), may hold values from 0 to 3840
Outputs:
- image: float32 [128, 262144], P(None, ('slab', 'det'))
Inputs may be any that keep to these rules, and one draw needn't show every extreme that they name: For detector d with home slab g = d // 4: max(0, g - 3) <= slab_range[d, 0] <= g <= slab_range[d, 1] <= min(127, g + 3); some detectors reach the full 3 on both sides where the grid allows.
All inputs are finite; a program needn't handle non-finite values.
Results may differ from a plain program's by a relative error of at most 0.007.
Values may be sent and summed in bfloat16 or wider, within the bound.
A program may use at most 64 MiB of HBM per device.

v0:
```python
import jax
import jax.numpy as jnp
from jax import lax
from jax.sharding import PartitionSpec as P

KWIN = 256
NTAB = 4
RANGE = 3


def shifted(x, axis, by):
    peers = lax.axis_size(axis)
    pairs = [(i, i + by) for i in range(peers) if 0 <= i + by < peers]
    return lax.ppermute(x, axis, pairs)


def from_everyone(x, axis):
    copies = jnp.broadcast_to(x, (lax.axis_size(axis), *x.shape))
    return lax.all_to_all(copies, axis, split_axis=0, concat_axis=0, tiled=True)


def joined_along(pieces, dim):
    shape = list(pieces.shape[1:])
    shape[dim] *= pieces.shape[0]
    return jnp.moveaxis(pieces, 0, dim).reshape(shape)


def collect(x, axis, dim):
    pieces = from_everyone(x, axis)
    return joined_along(pieces, dim)


def cut_windows(trace_rows, starts):

    def single(trace_row, first_index):
        return lax.dynamic_slice_in_dim(trace_row, first_index, KWIN, 1)

    return jax.vmap(single)(trace_rows, starts)


def bin_windows(windows, slot_ids, active):
    onehot = (slot_ids[:, None] == jnp.arange(NTAB, dtype=jnp.int32)[None, :]) & active[:, None]
    onehot = onehot.astype(jnp.bfloat16)
    return jnp.einsum("it,ifk->tfk", onehot, windows, preferred_element_type=jnp.float32)


def body(traces, tables, slab_range, table_slot, sample_start):
    position = lax.axis_index("slab")
    samples = traces.astype(jnp.bfloat16)
    own_active = (slab_range[:, 0] <= position) & (position <= slab_range[:, 1])
    stacked = bin_windows(
        cut_windows(samples, sample_start[:, RANGE]), table_slot[:, RANGE], own_active
    )
    for offset in list(range(-RANGE, 0)) + list(range(1, RANGE + 1)):
        target = position + offset
        active = (slab_range[:, 0] <= target) & (target <= slab_range[:, 1])
        windows = cut_windows(samples, sample_start[:, offset + RANGE])
        windows = windows * active[:, None, None].astype(jnp.bfloat16)
        arrived_windows, arrived_slots = shifted(
            (windows, table_slot[:, offset + RANGE]), "slab", offset
        )
        everything = jnp.ones(arrived_slots.shape, jnp.bool_)
        stacked = stacked + bin_windows(arrived_windows, arrived_slots, everything)
    binned = stacked.astype(jnp.bfloat16)
    return jnp.einsum(
        "btfk,tkv->fv", collect(binned[None], "det", 0), tables, preferred_element_type=jnp.float32
    )


def solution(mesh):
    placed = (
        P(("slab", "det"), None, None),
        P("slab", None, "det"),
        P(("slab", "det"), None),
        P(("slab", "det"), None),
        P(("slab", "det"), None),
    )
    return jax.shard_map(
        body, mesh=mesh, in_specs=placed, out_specs=P(None, ("slab", "det")), check_vma=False
    )
```

profile of v0, /device:TPU:9, one launch (start us, length us, event | category | flops | bytes accessed | tf_op | source)
XLA Modules:
  0.0 148.1 jit_solution(11387558839534990481)
XLA Ops:
  0.0 0.0 copy-start
  0.0 1.6 %fusion.7 = (s32[1,1]{1,0:T(1,128)}, s32[1,1]{1,0:T(1,128)}, s32[1,1]{1,0:T(1,128)}, s32[1,1]{1,0:T(1,128)}, s32[1,1]{1,0:T(1,128)}, /*index=5*/s32[1,1]{1,0:T(1,128)}, s32[1,1]{1,0:T(1,128)}) fusion(s32[1,7]{1,0:T(1,128)} %param.8), kind=kLoop, calls=%fused_computation.30 | loop fusion | bytes 56 | tf_op jit(solution)/shard_map/slice | solution.py:52
  1.6 3.7 %collective-permute-start.6 = (s32[1]{0:T(128)}, s32[1]{0:T(128)}, u32[]{:S(2)}, u32[]{:S(2)}) collective-permute-start(s32[1]{0:T(128)} %bitcast.33), channel_id=1, source_target_pairs={{0,4},{4,8},{8,12},{12,16},{16,20},{20,24},{24,28},{28,32},{32,36}... | collective-permute-start | bytes 20 | tf_op jit(solution)/shard_map/ppermute | solution.py:14
  5.3 1.9 %collective-permute-start.4 = (s32[1]{0:T(128)}, s32[1]{0:T(128)}, u32[]{:S(2)}, u32[]{:S(2)}) collective-permute-start(s32[1]{0:T(128)} %bitcast.25), channel_id=1, source_target_pairs={{4,0},{8,4},{12,8},{16,12},{20,16},{24,20},{28,24},{32,28},{36,32}... | collective-permute-start | bytes 20 | tf_op jit(solution)/shard_map/ppermute | solution.py:14
  7.2 4.3 %collective-permute-start.2 = (s32[1]{0:T(128)}, s32[1]{0:T(128)}, u32[]{:S(2)}, u32[]{:S(2)}) collective-permute-start(s32[1]{0:T(128)} %bitcast.17), channel_id=1, source_target_pairs={{8,0},{12,4},{16,8},{20,12},{24,16},{28,20},{32,24},{36,28},{40,32... | collective-permute-start | bytes 20 | tf_op jit(solution)/shard_map/ppermute | solution.py:14
  11.5 3.3 %collective-permute-start = (s32[1]{0:T(128)}, s32[1]{0:T(128)}, u32[]{:S(2)}, u32[]{:S(2)}) collective-permute-start(s32[1]{0:T(128)} %bitcast.9), channel_id=1, source_target_pairs={{12,0},{16,4},{20,8},{24,12},{28,16},{32,20},{36,24},{40,28},{44,3... | collective-permute-start | bytes 20 | tf_op jit(solution)/shard_map/ppermute | solution.py:14
  14.8 3.8 %collective-permute-start.10 = (s32[1]{0:T(128)}, s32[1]{0:T(128)}, u32[]{:S(2)}, u32[]{:S(2)}) collective-permute-start(s32[1]{0:T(128)} %bitcast.49), channel_id=1, source_target_pairs={{0,12},{4,16},{8,20},{12,24},{16,28},{20,32},{24,36},{28,40},{32,4... | collective-permute-start | bytes 20 | tf_op jit(solution)/shard_map/ppermute | solution.py:14
  18.6 1.3 fusion.9
  29.1 1.6 %fusion.8 = (s32[1,1]{1,0:T(1,128)}, s32[1,1]{1,0:T(1,128)}, s32[1,1]{1,0:T(1,128)}, s32[1,1]{1,0:T(1,128)}, s32[1,1]{1,0:T(1,128)}, /*index=5*/s32[1,1]{1,0:T(1,128)}, s32[1,1]{1,0:T(1,128)}) fusion(s32[1,7]{1,0:T(1,128)} %param.9), kind=kLoop, calls=%fused_computation.31 | loop fusion | bytes 56 | tf_op jit(solution)/shard_map/slice | solution.py:52
  39.6 1.7 %convert_element_type.13 = bf16[1,128,4096]{2,1,0:T(8,128)(2,1)S(1)} convert(f32[1,128,4096]{2,1,0:T(8,128)} %param.5) | non-fusion elementwise | flops 524288 | bytes 3145728 | tf_op jit(solution)/shard_map/convert_element_type | solution.py:49
  41.3 0.7 fusion
  46.4 0.2 bitcast_convert_fusion.6
  46.6 0.0 collective-permute-done.6
  46.6 1.9 %collective-permute-start.8 = (s32[1]{0:T(128)}, s32[1]{0:T(128)}, u32[]{:S(2)}, u32[]{:S(2)}) collective-permute-start(s32[1]{0:T(128)} %bitcast.41), channel_id=1, source_target_pairs={{0,8},{4,12},{8,16},{12,20},{16,24},{20,28},{24,32},{28,36},{32,40... | collective-permute-start | bytes 20 | tf_op jit(solution)/shard_map/ppermute | solution.py:14
  48.5 0.6 fusion.4
  49.2 0.0 collective-permute-done.4
  49.2 5.4 %collective-permute-start.11 = (bf16[1,128,256]{2,1,0:T(8,128)(2,1)S(1)}, bf16[1,128,256]{2,1,0:T(8,128)(2,1)S(1)}, u32[]{:S(2)}, u32[]{:S(2)}) collective-permute-start(bf16[1,128,256]{2,1,0:T(8,128)(2,1)S(1)} %get-tuple-element.83), channel_id=1, source_target_pairs={{0,12},{4,16},{8,20},{12,24},{16,28},{20,32},{24,36},{28,40},{32,4... | collective-permute-start | bytes 196616 | tf_op jit(solution)/shard_map/ppermute | solution.py:14
  54.6 0.6 fusion.3
  55.3 0.0 collective-permute-done.2
  55.3 2.2 %collective-permute-start.9 = (bf16[1,128,256]{2,1,0:T(8,128)(2,1)S(1)}, bf16[1,128,256]{2,1,0:T(8,128)(2,1)S(1)}, u32[]{:S(2)}, u32[]{:S(2)}) collective-permute-start(bf16[1,128,256]{2,1,0:T(8,128)(2,1)S(1)} %get-tuple-element.84), channel_id=1, source_target_pairs={{0,8},{4,12},{8,16},{12,20},{16,24},{20,28},{24,32},{28,36},{32,40... | collective-permute-start | bytes 196616 | tf_op jit(solution)/shard_map/ppermute | solution.py:14
  57.5 0.6 fusion.2
  58.1 0.0 collective-permute-done
  58.1 3.2 %collective-permute-start.7 = (bf16[1,128,256]{2,1,0:T(8,128)(2,1)S(1)}, bf16[1,128,256]{2,1,0:T(8,128)(2,1)S(1)}, u32[]{:S(2)}, u32[]{:S(2)}) collective-permute-start(bf16[1,128,256]{2,1,0:T(8,128)(2,1)S(1)} %get-tuple-element.85), channel_id=1, source_target_pairs={{0,4},{4,8},{8,12},{12,16},{16,20},{20,24},{24,28},{28,32},{32,36}... | collective-permute-start | bytes 196616 | tf_op jit(solution)/shard_map/ppermute | solution.py:14
  61.3 0.6 fusion.1
  62.0 0.0 collective-permute-done.10
  62.0 1.9 %collective-permute-start.5 = (bf16[1,128,256]{2,1,0:T(8,128)(2,1)S(1)}, bf16[1,128,256]{2,1,0:T(8,128)(2,1)S(1)}, u32[]{:S(2)}, u32[]{:S(2)}) collective-permute-start(bf16[1,128,256]{2,1,0:T(8,128)(2,1)S(1)} %get-tuple-element.86), channel_id=1, source_target_pairs={{4,0},{8,4},{12,8},{16,12},{20,16},{24,20},{28,24},{32,28},{36,32}... | collective-permute-start | bytes 196616 | tf_op jit(solution)/shard_map/ppermute | solution.py:14
  63.9 0.6 fusion.6
  64.5 0.0 collective-permute-done.8
  64.5 4.4 %collective-permute-start.3 = (bf16[1,128,256]{2,1,0:T(8,128)(2,1)S(1)}, bf16[1,128,256]{2,1,0:T(8,128)(2,1)S(1)}, u32[]{:S(2)}, u32[]{:S(2)}) collective-permute-start(bf16[1,128,256]{2,1,0:T(8,128)(2,1)S(1)} %get-tuple-element.87), channel_id=1, source_target_pairs={{8,0},{12,4},{16,8},{20,12},{24,16},{28,20},{32,24},{36,28},{40,32... | collective-permute-start | bytes 196616 | tf_op jit(solution)/shard_map/ppermute | solution.py:14
  68.9 0.7 fusion.5
  69.6 0.0 collective-permute-done.11
  69.6 1.9 %collective-permute-start.1 = (bf16[1,128,256]{2,1,0:T(8,128)(2,1)S(1)}, bf16[1,128,256]{2,1,0:T(8,128)(2,1)S(1)}, u32[]{:S(2)}, u32[]{:S(2)}) collective-permute-start(bf16[1,128,256]{2,1,0:T(8,128)(2,1)S(1)} %get-tuple-element.88), channel_id=1, source_target_pairs={{12,0},{16,4},{20,8},{24,12},{28,16},{32,20},{36,24},{40,28},{44,3... | collective-permute-start | bytes 196616 | tf_op jit(solution)/shard_map/ppermute | solution.py:14
  71.6 0.0 collective-permute-done.9
  71.6 0.0 collective-permute-done.7
  71.6 0.0 collective-permute-done.5
  71.6 0.0 collective-permute-done.3
  71.7 5.0 %collective-permute-done.1 = bf16[1,128,256]{2,1,0:T(8,128)(2,1)S(1)} collective-permute-done((bf16[1,128,256]{2,1,0:T(8,128)(2,1)S(1)}, bf16[1,128,256]{2,1,0:T(8,128)(2,1)S(1)}, u32[]{:S(2)}, u32[]{:S(2)}) %collective-permute-start.1) | collective-permute-done | bytes 65568 | tf_op jit(solution)/shard_map/ppermute | solution.py:14
  76.7 0.3 add_convert_fusion
  77.0 0.1 broadcast_in_dim.23
  77.1 69.9 %all_to_all.5 = bf16[4,1,4,128,256]{4,3,2,1,0:T(8,128)(2,1)S(1)} all-to-all(bf16[4,1,4,128,256]{4,3,2,1,0:T(8,128)(2,1)S(1)} %broadcast_in_dim.23), channel_id=1, replica_groups=mesh['slab'=128,'det'=4] {'det'}, dimensions={0} | all-to-all | bytes 2097152 | tf_op jit(solution)/shard_map/all_to_all | solution.py:19
  147.0 0.1 convert_reduce_fusion
  147.1 0.0 copy-done
  147.1 1.0 convolution_bitcast_fusion
  (6 shorter events, 0.1 us)
Async XLA Ops:
  0.0 147.1 %copy-start = (bf16[4,256,512]{2,1,0:T(8,128)(2,1)S(1)}, bf16[4,256,512]{2,1,0:T(8,128)(2,1)}, u32[]{:S(2)}) copy-start(bf16[4,256,512]{2,1,0:T(8,128)(2,1)} %param.6) | copy-start | bytes 3145732
  1.6 45.0 %collective-permute-start.6 = (s32[1]{0:T(128)}, s32[1]{0:T(128)}, u32[]{:S(2)}, u32[]{:S(2)}) collective-permute-start(s32[1]{0:T(128)} %bitcast.33), channel_id=1, source_target_pairs={{0,4},{4,8},{8,12},{12,16},{16,20},{20,24},{24,28},{28,32},{32,36}... | collective-permute-start | bytes 20 | tf_op jit(solution)/shard_map/ppermute | solution.py:14
  5.3 43.9 %collective-permute-start.4 = (s32[1]{0:T(128)}, s32[1]{0:T(128)}, u32[]{:S(2)}, u32[]{:S(2)}) collective-permute-start(s32[1]{0:T(128)} %bitcast.25), channel_id=1, source_target_pairs={{4,0},{8,4},{12,8},{16,12},{20,16},{24,20},{28,24},{32,28},{36,32}... | collective-permute-start | bytes 20 | tf_op jit(solution)/shard_map/ppermute | solution.py:14
  7.2 48.1 %collective-permute-start.2 = (s32[1]{0:T(128)}, s32[1]{0:T(128)}, u32[]{:S(2)}, u32[]{:S(2)}) collective-permute-start(s32[1]{0:T(128)} %bitcast.17), channel_id=1, source_target_pairs={{8,0},{12,4},{16,8},{20,12},{24,16},{28,20},{32,24},{36,28},{40,32... | collective-permute-start | bytes 20 | tf_op jit(solution)/shard_map/ppermute | solution.py:14
  11.5 46.6 %collective-permute-start = (s32[1]{0:T(128)}, s32[1]{0:T(128)}, u32[]{:S(2)}, u32[]{:S(2)}) collective-permute-start(s32[1]{0:T(128)} %bitcast.9), channel_id=1, source_target_pairs={{12,0},{16,4},{20,8},{24,12},{28,16},{32,20},{36,24},{40,28},{44,3... | collective-permute-start | bytes 20 | tf_op jit(solution)/shard_map/ppermute | solution.py:14
  14.8 47.2 %collective-permute-start.10 = (s32[1]{0:T(128)}, s32[1]{0:T(128)}, u32[]{:S(2)}, u32[]{:S(2)}) collective-permute-start(s32[1]{0:T(128)} %bitcast.49), channel_id=1, source_target_pairs={{0,12},{4,16},{8,20},{12,24},{16,28},{20,32},{24,36},{28,40},{32,4... | collective-permute-start | bytes 20 | tf_op jit(solution)/shard_map/ppermute | solution.py:14
  46.6 17.9 %collective-permute-start.8 = (s32[1]{0:T(128)}, s32[1]{0:T(128)}, u32[]{:S(2)}, u32[]{:S(2)}) collective-permute-start(s32[1]{0:T(128)} %bitcast.41), channel_id=1, source_target_pairs={{0,8},{4,12},{8,16},{12,20},{16,24},{20,28},{24,32},{28,36},{32,40... | collective-permute-start | bytes 20 | tf_op jit(solution)/shard_map/ppermute | solution.py:14
  49.2 20.4 %collective-permute-start.11 = (bf16[1,128,256]{2,1,0:T(8,128)(2,1)S(1)}, bf16[1,128,256]{2,1,0:T(8,128)(2,1)S(1)}, u32[]{:S(2)}, u32[]{:S(2)}) collective-permute-start(bf16[1,128,256]{2,1,0:T(8,128)(2,1)S(1)} %get-tuple-element.83), channel_id=1, source_target_pairs={{0,12},{4,16},{8,20},{12,24},{16,28},{20,32},{24,36},{28,40},{32,4... | collective-permute-start | bytes 196616 | tf_op jit(solution)/shard_map/ppermute | solution.py:14
  55.3 16.3 %collective-permute-start.9 = (bf16[1,128,256]{2,1,0:T(8,128)(2,1)S(1)}, bf16[1,128,256]{2,1,0:T(8,128)(2,1)S(1)}, u32[]{:S(2)}, u32[]{:S(2)}) collective-permute-start(bf16[1,128,256]{2,1,0:T(8,128)(2,1)S(1)} %get-tuple-element.84), channel_id=1, source_target_pairs={{0,8},{4,12},{8,16},{12,20},{16,24},{20,28},{24,32},{28,36},{32,40... | collective-permute-start | bytes 196616 | tf_op jit(solution)/shard_map/ppermute | solution.py:14
  58.1 13.4 %collective-permute-start.7 = (bf16[1,128,256]{2,1,0:T(8,128)(2,1)S(1)}, bf16[1,128,256]{2,1,0:T(8,128)(2,1)S(1)}, u32[]{:S(2)}, u32[]{:S(2)}) collective-permute-start(bf16[1,128,256]{2,1,0:T(8,128)(2,1)S(1)} %get-tuple-element.85), channel_id=1, source_target_pairs={{0,4},{4,8},{8,12},{12,16},{16,20},{20,24},{24,28},{28,32},{32,36}... | collective-permute-start | bytes 196616 | tf_op jit(solution)/shard_map/ppermute | solution.py:14
  62.0 9.7 %collective-permute-start.5 = (bf16[1,128,256]{2,1,0:T(8,128)(2,1)S(1)}, bf16[1,128,256]{2,1,0:T(8,128)(2,1)S(1)}, u32[]{:S(2)}, u32[]{:S(2)}) collective-permute-start(bf16[1,128,256]{2,1,0:T(8,128)(2,1)S(1)} %get-tuple-element.86), channel_id=1, source_target_pairs={{4,0},{8,4},{12,8},{16,12},{20,16},{24,20},{28,24},{32,28},{36,32}... | collective-permute-start | bytes 196616 | tf_op jit(solution)/shard_map/ppermute | solution.py:14
  64.5 7.2 %collective-permute-start.3 = (bf16[1,128,256]{2,1,0:T(8,128)(2,1)S(1)}, bf16[1,128,256]{2,1,0:T(8,128)(2,1)S(1)}, u32[]{:S(2)}, u32[]{:S(2)}) collective-permute-start(bf16[1,128,256]{2,1,0:T(8,128)(2,1)S(1)} %get-tuple-element.87), channel_id=1, source_target_pairs={{8,0},{12,4},{16,8},{20,12},{24,16},{28,20},{32,24},{36,28},{40,32... | collective-permute-start | bytes 196616 | tf_op jit(solution)/shard_map/ppermute | solution.py:14
  69.6 7.1 %collective-permute-start.1 = (bf16[1,128,256]{2,1,0:T(8,128)(2,1)S(1)}, bf16[1,128,256]{2,1,0:T(8,128)(2,1)S(1)}, u32[]{:S(2)}, u32[]{:S(2)}) collective-permute-start(bf16[1,128,256]{2,1,0:T(8,128)(2,1)S(1)} %get-tuple-element.88), channel_id=1, source_target_pairs={{12,0},{16,4},{20,8},{24,12},{28,16},{32,20},{36,24},{40,28},{44,3... | collective-permute-start | bytes 196616 | tf_op jit(solution)/shard_map/ppermute | solution.py:14
where the time goes:
time: 149 us; the launch traced here: 148 us
  blocking collectives  69.9 us (47%)
  starting transfers between devices  37.9 us (25%)
  between operations  22.8 us (15%)
  other arithmetic  6.93 us (5%)
  waiting for transfers between devices  5.04 us (3%)
  local copies, waits for them, and re-layouts  4.59 us (3%)
    all_to_all x1, blocking collectives, from_everyone(): return lax.all_to_all(copies, axis, split_axis=0, concat_axis=0, tiled=True)  69.9 us
    ppermute x12, starting transfers between devices, shifted(): return lax.ppermute(x, axis, pairs)  37.9 us
    ppermute x12, waiting for transfers between devices, shifted(): return lax.ppermute(x, axis, pairs)  5.04 us
    another operation x14, other arithmetic  4.77 us
  transfers between devices with their start and end apart: 12, of which 1 were waited for; matrix products, arithmetic and copies ran while one was open for 6% of the time, Pallas kernels for 0%

commit v1 on v0

v1 whole, which is shorter than its diff:
```python
import functools

import jax
import jax.numpy as jnp
from jax import lax
from jax.experimental import pallas as pl
from jax.experimental.pallas import tpu as pltpu
from jax.sharding import PartitionSpec as P

KWIN = 256
NTAB = 4
RANGE = 3
CHUNKS = 4
LANES = 128
MESH = pl.DeviceIdType.MESH
OFFSETS = [1, -1, 2, -2, 3, -3]


def kernel(
    n_slab, rows, span_ref, slot_ref, start_ref, traces_ref, tables_ref, out_ref,
    trace_v, moves, win, got, slots_out, slots_in, stack, part, full, land1, land2, land3, tab, out_v,
    load_sem, tab_sem, store_sem, slot_send, slot_recv, win_send, win_recv, z_send, z_recv,
):
    slab = lax.axis_index("slab")
    det = lax.axis_index("det")
    side = det + 1 - 2 * lax.rem(det, 2)
    across = 3 - det
    keep_a = lax.rem((det + 1) // 2, 2)
    keep_b = 2 + det // 2
    give_a = 1 - keep_a
    give_b = 5 - keep_b
    first = (side, across)
    second = (across, side)
    keeps = (keep_a, keep_b)
    gives = (give_a, give_b)

    def inside(s):
        return jnp.logical_and(s >= 0, s < n_slab)

    def piece(c):
        return pl.ds(c * rows, rows)

    n_tiles = trace_v.shape[0]

    @pl.loop(0, n_tiles)
    def _(tile):
        pltpu.make_async_copy(
            traces_ref.at[0, :, pl.ds(pl.multiple_of(tile * LANES, LANES), LANES)],
            trace_v.at[tile], load_sem,
        ).start()

    tab_load = pltpu.make_async_copy(tables_ref, tab, tab_sem)
    tab_load.start()

    barrier = pltpu.get_barrier_semaphore()
    friends = 2
    for peer in (side, across):
        pl.semaphore_signal(barrier, inc=1, device_id=(slab, peer), device_id_type=MESH)
    for o in OFFSETS:
        there = inside(slab + o)
        friends = friends + there.astype(jnp.int32)

        @pl.when(there)
        def _():
            pl.semaphore_signal(barrier, inc=1, device_id=(slab + o, det), device_id_type=MESH)

    flat = (8, LANES)
    low = jnp.full(flat, span_ref[0, 0], jnp.int32)
    high = jnp.full(flat, span_ref[0, 1], jnp.int32)
    for i in range(2 * RANGE + 1):
        target = slab + (i - RANGE)
        active = jnp.logical_and(low <= target, target <= high)
        slots_out[i] = jnp.where(active, jnp.full(flat, slot_ref[0, i], jnp.int32), -1)
    for o in OFFSETS:
        i = o + RANGE

        @pl.when(jnp.logical_not(inside(slab - o)))
        def _():
            slots_in[i] = jnp.full((8, LANES), -1, jnp.int32)
            got[i] = jnp.zeros((CHUNKS * rows, KWIN), jnp.bfloat16)

    down = lax.broadcasted_iota(jnp.int32, (2 * LANES, LANES), 0)
    along = lax.broadcasted_iota(jnp.int32, (2 * LANES, LANES), 1)
    for i in range(2 * RANGE + 1):
        shift = lax.rem(start_ref[0, i], LANES)
        moves[i] = jnp.where(down - along == shift, 1.0, 0.0).astype(jnp.bfloat16)

    def cut(i, c):
        tile = lax.div(start_ref[0, i], LANES)
        last = lax.min(tile + 2, n_tiles - 1)
        tiles = [trace_v[spot, piece(c), :].astype(jnp.bfloat16) for spot in (tile, tile + 1, last)]
        for h in range(2):
            pair = jnp.concatenate([tiles[h], tiles[h + 1]], axis=1)
            win[i, piece(c), pl.ds(h * LANES, LANES)] = jnp.dot(
                pair, moves[i], preferred_element_type=jnp.float32
            ).astype(jnp.bfloat16)

    def slot_copy(o):
        i = o + RANGE
        return pltpu.make_async_remote_copy(
            src_ref=slots_out.at[i], dst_ref=slots_in.at[i],
            send_sem=slot_send.at[i], recv_sem=slot_recv.at[i],
            device_id=(slab + o, det), device_id_type=MESH,
        )

    def win_copy(o, c):
        i = o + RANGE
        return pltpu.make_async_remote_copy(
            src_ref=win.at[i, piece(c), :], dst_ref=got.at[i, piece(c), :],
            send_sem=win_send.at[i, c], recv_sem=win_recv.at[i, c],
            device_id=(slab + o, det), device_id_type=MESH,
        )

    def z_copy(step, cls, c, src, dst, peer):
        return pltpu.make_async_remote_copy(
            src_ref=src, dst_ref=dst,
            send_sem=z_send.at[step, cls, c], recv_sem=z_recv.at[step, cls, c],
            device_id=(slab, peer), device_id_type=MESH,
        )

    def step1(cls, c):
        return z_copy(
            0, cls, c, stack.at[gives[cls], piece(c), :], land1.at[cls, piece(c), :], first[cls]
        )

    def step2(cls, c):
        return z_copy(
            1, cls, c, part.at[cls, piece(c), :], land2.at[cls, piece(c), :], second[cls]
        )

    def step3(cls, c):
        return z_copy(
            2, cls, c, full.at[cls, piece(c), :], land3.at[cls, piece(c), :], first[cls]
        )

    pltpu.make_async_copy(trace_v, trace_v, load_sem).wait()
    for c in range(CHUNKS):
        for i in range(2 * RANGE + 1):
            cut(i, c)
        if c == 0:
            pl.semaphore_wait(barrier, friends)
            for o in OFFSETS:

                @pl.when(inside(slab + o))
                def _():
                    slot_copy(o).start()

        for o in OFFSETS:

            @pl.when(inside(slab + o))
            def _():
                win_copy(o, c).start()

    for o in OFFSETS:

        @pl.when(inside(slab - o))
        def _():
            slot_copy(o).wait_recv()

    for c in range(CHUNKS):
        for o in OFFSETS:

            @pl.when(inside(slab - o))
            def _():
                win_copy(o, c).wait_recv()

        for h in range(2):
            cols = pl.ds(h * LANES, LANES)
            sums = [jnp.zeros((rows, LANES), jnp.float32) for _ in range(NTAB)]
            for o in [0, *OFFSETS]:
                i = o + RANGE
                source, slots = (win, slots_out) if o == 0 else (got, slots_in)
                window = source[i, piece(c), cols].astype(jnp.float32)
                block = jnp.broadcast_to(slots[i, 0:1, :], (rows, LANES))
                for t in range(NTAB):
                    sums[t] = sums[t] + jnp.where(block == t, window, 0.0)
            for t in range(NTAB):
                stack[t, piece(c), cols] = sums[t].astype(jnp.bfloat16)
        for cls in range(2):
            step1(cls, c).start()

    for c in range(CHUNKS):
        for cls in range(2):
            step1(cls, c).wait_recv()
            mine = stack[keeps[cls], piece(c), :].astype(jnp.float32)
            theirs = land1[cls, piece(c), :].astype(jnp.float32)
            part[cls, piece(c), :] = (mine + theirs).astype(jnp.bfloat16)
            step2(cls, c).start()

    for c in range(CHUNKS):
        for cls in range(2):
            step2(cls, c).wait_recv()
            mine = part[cls, piece(c), :].astype(jnp.float32)
            theirs = land2[cls, piece(c), :].astype(jnp.float32)
            full[cls, piece(c), :] = (mine + theirs).astype(jnp.bfloat16)
            step3(cls, c).start()

    tab_load.wait()
    out_v[...] = jnp.dot(
        full[0], tab[keeps[0]], preferred_element_type=jnp.float32
    ) + jnp.dot(full[1], tab[keeps[1]], preferred_element_type=jnp.float32)
    stores = []
    for c in range(CHUNKS):
        total = out_v[piece(c), :]
        for cls in range(2):
            step3(cls, c).wait_recv()
            total = total + jnp.dot(
                land3[cls, piece(c), :], tab[gives[cls]], preferred_element_type=jnp.float32
            )
        out_v[piece(c), :] = total
        store = pltpu.make_async_copy(
            out_v.at[piece(c), :], out_ref.at[piece(c), :], store_sem.at[c]
        )
        store.start()
        stores.append(store)

    for o in OFFSETS:

        @pl.when(inside(slab + o))
        def _():
            slot_copy(o).wait_send()
            for c in range(CHUNKS):
                win_copy(o, c).wait_send()

    for c in range(CHUNKS):
        for cls in range(2):
            step1(cls, c).wait_send()
            step2(cls, c).wait_send()
            step3(cls, c).wait_send()
        stores[c].wait()


def body(n_slab, traces, tables, slab_range, table_slot, sample_start):
    _, frames, samp = traces.shape
    vox = tables.shape[2]
    rows = frames // CHUNKS
    reach = 2 * RANGE + 1
    smem = pl.BlockSpec(memory_space=pltpu.SMEM)
    far = pl.BlockSpec(memory_space=pl.ANY)
    half = pltpu.VMEM((2, frames, KWIN), jnp.bfloat16)
    dma = pltpu.SemaphoreType.DMA
    return pl.pallas_call(
        functools.partial(kernel, n_slab, rows),
        out_shape=jax.ShapeDtypeStruct((frames, vox), jnp.float32),
        in_specs=[smem, smem, smem, far, far],
        out_specs=far,
        scratch_shapes=[
            pltpu.VMEM((samp // LANES, frames, LANES), jnp.float32),
            pltpu.VMEM((reach, 2 * LANES, LANES), jnp.bfloat16),
            pltpu.VMEM((reach, frames, KWIN), jnp.bfloat16),
            pltpu.VMEM((reach, frames, KWIN), jnp.bfloat16),
            pltpu.VMEM((reach, 8, LANES), jnp.int32),
            pltpu.VMEM((reach, 8, LANES), jnp.int32),
            pltpu.VMEM((NTAB, frames, KWIN), jnp.bfloat16),
            half, half, half, half, half,
            pltpu.VMEM((NTAB, KWIN, vox), jnp.bfloat16),
            pltpu.VMEM((frames, vox), jnp.float32),
            dma, dma, dma((CHUNKS,)),
            dma((reach,)), dma((reach,)),
            dma((reach, CHUNKS)), dma((reach, CHUNKS)),
            dma((3, 2, CHUNKS)), dma((3, 2, CHUNKS)),
        ],
        compiler_params=pltpu.CompilerParams(collective_id=0, has_side_effects=True),
    )(slab_range, table_slot, sample_start, traces, tables)


def solution(mesh):
    placed = (
        P(("slab", "det"), None, None),
        P("slab", None, "det"),
        P(("slab", "det"), None),
        P(("slab", "det"), None),
        P(("slab", "det"), None),
    )
    return jax.shard_map(
        functools.partial(body, mesh.shape["slab"]),
        mesh=mesh, in_specs=placed, out_specs=P(None, ("slab", "det")), check_vma=False,
    )
```

time: 149 us -> 46 us (0.31)
  the two profiles are of different devices: /device:TPU:9 before, /device:TPU:32 now
where the time goes in v1:
time: 46 us; the launch traced here: 45.8 us
  Pallas kernels  44.1 us (96%)
  local copies, waits for them, and re-layouts  1.67 us (4%)
    pallas_call x1, Pallas kernels, body(): pl.pallas_call(functools.partial(kernel, n_slab, rows), out_shape=jax.Sha...  44.1 us
    unnamed x1, local copies, waits for them, and re-layouts  1.67 us

profile of v1, /device:TPU:32, one launch (start us, length us, event | category | flops | bytes accessed | tf_op | source)
XLA Modules:
  0.0 45.8 jit_solution(11522797555170486544)
XLA Ops:
  0.0 44.1 %shard_map.55 = f32[128,512]{1,0:T(8,128)} custom-call(s32[1,2]{1,0:T(1,128)} %span_ref.1, s32[1,7]{1,0:T(1,128)} %slot_ref.1, s32[1,7]{1,0:T(1,128)} %start_ref.1, f32[1,128,4096]{2,1,0:T(8,128)} %traces_ref.1, bf16[4,256,512]{2,1,0:T(8,128)(2,1)} %tables_ref.1), custom_call_target="tpu_custom_call" | custom-call | tf_op jit(solution)/shard_map/pallas_call | solution.py:242
  44.1 1.7 %copy.7 = f32[128,512]{1,0:T(8,128)} copy(f32[128,512]{1,0:T(8,128)} %shard_map.55) | data formatting | bytes 524288

commit v2 on v0

v2 whole, which is shorter than its diff:
```python
import functools

import jax
import jax.numpy as jnp
from jax import lax
from jax.experimental import pallas as pl
from jax.experimental.pallas import tpu as pltpu
from jax.sharding import PartitionSpec as P

KWIN = 256
NTAB = 4
RANGE = 3
REACH = 2 * RANGE + 1
SIZES = (16, 16, 32, 32, 32)
CHUNKS = len(SIZES)
LANES = 128
MESH = pl.DeviceIdType.MESH
OFFSETS = [3, -3, 2, -2, 1, -1]


def kernel(
    n_slab, traces_ref, tables_ref, span_hbm, slot_hbm, start_hbm, out_ref,
    span_ref, slot_ref, start_ref, trace_v, moves, win, got, slots_out, slots_in,
    stack, sums, land, tab,
    int_sem, load_sem, tab_sem, slot_send, slot_recv, win_send, win_recv, z_send, z_recv, hello,
):
    slab = lax.axis_index("slab")
    det = lax.axis_index("det")
    side = det + 1 - 2 * lax.rem(det, 2)
    across = 3 - det
    keep_a = lax.rem((det + 1) // 2, 2)
    keep_b = 2 + det // 2
    first = (side, across)
    second = (across, side)
    keeps = (keep_a, keep_b)
    gives = (1 - keep_a, 5 - keep_b)
    n_tiles = trace_v.shape[0]
    near = jnp.minimum(slab, RANGE) + jnp.minimum(n_slab - 1 - slab, RANGE)

    def inside(s):
        return jnp.logical_and(s >= 0, s < n_slab)

    def piece(c):
        return pl.ds(sum(SIZES[:c]), SIZES[c])

    def wait_bytes(ref, sem):
        pltpu.make_async_copy(ref, ref, sem).wait()

    def wait_near(refs, sem):
        for n in range(RANGE, 2 * RANGE + 1):

            @pl.when(near == n)
            def _():
                wait_bytes(refs(n), sem)

    barrier = pltpu.get_barrier_semaphore()
    greets_side = jnp.logical_or(det == 0, det == 3)
    greets_across = det < 2
    friends = near + jnp.where(det == 2, 2, jnp.where(det == 0, 0, 1))

    @pl.when(greets_side)
    def _():
        pl.semaphore_signal(barrier, inc=1, device_id=(slab, side), device_id_type=MESH)

    @pl.when(greets_across)
    def _():
        pl.semaphore_signal(barrier, inc=1, device_id=(slab, across), device_id_type=MESH)

    for o in OFFSETS:

        @pl.when(inside(slab + o))
        def _():
            pl.semaphore_signal(barrier, inc=1, device_id=(slab + o, det), device_id_type=MESH)

    ints = [
        pltpu.make_async_copy(src, dst, int_sem.at[n])
        for n, (src, dst) in enumerate(
            [(start_hbm, start_ref), (span_hbm, span_ref), (slot_hbm, slot_ref)]
        )
    ]
    for copy in ints:
        copy.start()

    @pl.loop(0, n_tiles)
    def _(tile):
        pltpu.make_async_copy(
            traces_ref.at[0, :, pl.ds(pl.multiple_of(tile * LANES, LANES), LANES)],
            trace_v.at[tile], load_sem,
        ).start()

    tab_load = pltpu.make_async_copy(tables_ref, tab, tab_sem)

    for copy in ints:
        copy.wait()

    flat = (8, LANES)
    low = jnp.full(flat, span_ref[0, 0], jnp.int32)
    high = jnp.full(flat, span_ref[0, 1], jnp.int32)
    for q, o in enumerate([*OFFSETS, 0]):
        target = slab + o
        active = jnp.logical_and(low <= target, target <= high)
        slots_out[q] = jnp.where(active, jnp.full(flat, slot_ref[0, o + RANGE], jnp.int32), -1)
    for q, o in enumerate(OFFSETS):

        @pl.when(jnp.logical_not(inside(slab - o)))
        def _():
            slots_in[q] = jnp.full(flat, -1, jnp.int32)
            got[q] = jnp.zeros(got.shape[1:], jnp.bfloat16)

    down = lax.broadcasted_iota(jnp.int32, (2 * LANES, LANES), 0)
    along = lax.broadcasted_iota(jnp.int32, (2 * LANES, LANES), 1)
    for q, o in enumerate([*OFFSETS, 0]):
        shift = lax.rem(start_ref[0, o + RANGE], LANES)
        moves[q] = jnp.where(down - along == shift, 1.0, 0.0).astype(jnp.bfloat16)

    def cut(q, o, c):
        tile = lax.div(start_ref[0, o + RANGE], LANES)
        last = lax.min(tile + 2, n_tiles - 1)
        tiles = [trace_v[spot, piece(c), :].astype(jnp.bfloat16) for spot in (tile, tile + 1, last)]
        for h in range(2):
            pair = jnp.concatenate([tiles[h], tiles[h + 1]], axis=1)
            win[q, piece(c), pl.ds(h * LANES, LANES)] = jnp.dot(
                pair, moves[q], preferred_element_type=jnp.float32
            ).astype(jnp.bfloat16)

    def send(src, dst, send_sem, recv_sem, where):
        pltpu.make_async_remote_copy(
            src_ref=src, dst_ref=dst, send_sem=send_sem, recv_sem=recv_sem,
            device_id=where, device_id_type=MESH,
        ).start()

    def send_step(step, c):
        for cls in range(2):
            src = stack.at[gives[cls]] if step == 0 else sums.at[step - 1, cls]
            send(
                src.at[piece(c), :], land.at[step, cls, piece(c), :],
                z_send, z_recv.at[step, c],
                (slab, (second if step == 1 else first)[cls]),
            )

    def wait_step(step, c):
        wait_bytes(land.at[step, :, piece(c), :], z_recv.at[step, c])

    wait_bytes(trace_v, load_sem)
    tab_load.start()
    for c in range(CHUNKS):
        for q, o in enumerate([*OFFSETS, 0]):
            cut(q, o, c)
        if c == 0:
            pl.semaphore_wait(barrier, friends)

            @pl.when(jnp.logical_not(greets_side))
            def _():
                pl.semaphore_signal(
                    hello.at[0], inc=1, device_id=(slab, side), device_id_type=MESH
                )

            @pl.when(jnp.logical_not(greets_across))
            def _():
                pl.semaphore_signal(
                    hello.at[1], inc=1, device_id=(slab, across), device_id_type=MESH
                )

        for q, o in enumerate(OFFSETS):

            @pl.when(inside(slab + o))
            def _():
                if c == 0:
                    send(slots_out.at[q], slots_in.at[q], slot_send, slot_recv, (slab + o, det))
                send(
                    win.at[q, piece(c), :], got.at[q, piece(c), :],
                    win_send, win_recv.at[c], (slab + o, det),
                )

    wait_near(lambda n: slots_in.at[pl.ds(0, n)], slot_recv)
    for c in range(CHUNKS):
        wait_near(lambda n: got.at[pl.ds(0, n), piece(c), :], win_recv.at[c])

        rows = SIZES[c]
        for h in range(2):
            cols = pl.ds(h * LANES, LANES)
            bins = [jnp.zeros((rows, LANES), jnp.float32) for _ in range(NTAB)]
            for q, o in enumerate([*OFFSETS, 0]):
                source, slots = (win, slots_out) if o == 0 else (got, slots_in)
                window = source[q, piece(c), cols].astype(jnp.float32)
                block = jnp.broadcast_to(slots[q, 0:1, :], (rows, LANES))
                for t in range(NTAB):
                    bins[t] = bins[t] + jnp.where(block == t, window, 0.0)
            for t in range(NTAB):
                stack[t, piece(c), cols] = bins[t].astype(jnp.bfloat16)
        if c == 0:
            @pl.when(greets_side)
            def _():
                pl.semaphore_wait(hello.at[0], 1)

            @pl.when(greets_across)
            def _():
                pl.semaphore_wait(hello.at[1], 1)

        send_step(0, c)

    for step in range(2):
        for c in range(CHUNKS):
            wait_step(step, c)
            for cls in range(2):
                mine = stack[keeps[cls], piece(c), :] if step == 0 else sums[0, cls, piece(c), :]
                theirs = land[step, cls, piece(c), :]
                sums[step, cls, piece(c), :] = (
                    mine.astype(jnp.float32) + theirs.astype(jnp.float32)
                ).astype(jnp.bfloat16)
            send_step(step + 1, c)

    wait_bytes(tab, tab_sem)
    out_ref[...] = jnp.dot(
        sums[1, 0], tab[keeps[0]], preferred_element_type=jnp.float32
    ) + jnp.dot(sums[1, 1], tab[keeps[1]], preferred_element_type=jnp.float32)
    for c in range(CHUNKS):
        wait_step(2, c)
        total = out_ref[piece(c), :]
        for cls in range(2):
            total = total + jnp.dot(
                land[2, cls, piece(c), :], tab[gives[cls]], preferred_element_type=jnp.float32
            )
        out_ref[piece(c), :] = total

    wait_near(lambda n: slots_out.at[pl.ds(0, n)], slot_send)
    wait_near(lambda n: win.at[pl.ds(0, n)], win_send)
    wait_bytes(land, z_send)


def body(n_slab, traces, tables, slab_range, table_slot, sample_start):
    _, frames, samp = traces.shape
    vox = tables.shape[2]
    far = pl.BlockSpec(memory_space=pl.ANY)
    dma = pltpu.SemaphoreType.DMA
    return pl.pallas_call(
        functools.partial(kernel, n_slab),
        out_shape=pltpu.VMEM((frames, vox), jnp.float32),
        in_specs=[far] * 5,
        out_specs=pl.BlockSpec(memory_space=pltpu.VMEM),
        scratch_shapes=[
            pltpu.SMEM((1, 2), jnp.int32),
            pltpu.SMEM((1, REACH), jnp.int32),
            pltpu.SMEM((1, REACH), jnp.int32),
            pltpu.VMEM((samp // LANES, frames, LANES), jnp.float32),
            pltpu.VMEM((REACH, 2 * LANES, LANES), jnp.bfloat16),
            pltpu.VMEM((REACH, frames, KWIN), jnp.bfloat16),
            pltpu.VMEM((2 * RANGE, frames, KWIN), jnp.bfloat16),
            pltpu.VMEM((REACH, 8, LANES), jnp.int32),
            pltpu.VMEM((2 * RANGE, 8, LANES), jnp.int32),
            pltpu.VMEM((NTAB, frames, KWIN), jnp.bfloat16),
            pltpu.VMEM((2, 2, frames, KWIN), jnp.bfloat16),
            pltpu.VMEM((3, 2, frames, KWIN), jnp.bfloat16),
            pltpu.VMEM((NTAB, KWIN, vox), jnp.bfloat16),
            dma((3,)), dma, dma, dma, dma, dma, dma((CHUNKS,)), dma, dma((3, CHUNKS)),
            pltpu.SemaphoreType.REGULAR((2,)),
        ],
        compiler_params=pltpu.CompilerParams(collective_id=0, has_side_effects=True),
    )(traces, tables, slab_range, table_slot, sample_start)


def solution(mesh):
    placed = (
        P(("slab", "det"), None, None),
        P("slab", None, "det"),
        P(("slab", "det"), None),
        P(("slab", "det"), None),
        P(("slab", "det"), None),
    )
    return jax.shard_map(
        functools.partial(body, mesh.shape["slab"]),
        mesh=mesh, in_specs=placed, out_specs=P(None, ("slab", "det")), check_vma=False,
    )
```

time: 149 us -> 44.1 us (0.30)
  the two profiles are of different devices: /device:TPU:9 before, /device:TPU:30 now
where the time goes in v2:
time: 44.1 us; the launch traced here: 43.9 us
  Pallas kernels  43.2 us (98%)
  local copies, waits for them, and re-layouts  0.71 us (2%)
    pallas_call x1, Pallas kernels, body(): pl.pallas_call(functools.partial(kernel, n_slab), out_shape=pltpu.VMEM((f...  43.2 us

profile of v2, /device:TPU:30, one launch (start us, length us, event | category | flops | bytes accessed | tf_op | source)
XLA Modules:
  0.0 43.9 jit_solution(6723771693231059593)
XLA Ops:
  0.0 43.2 %shard_map.55 = f32[128,512]{1,0:T(8,128)S(1)} custom-call(f32[1,128,4096]{2,1,0:T(8,128)} %traces_ref.1, bf16[4,256,512]{2,1,0:T(8,128)(2,1)} %tables_ref.1, s32[1,2]{1,0:T(1,128)} %span_hbm.1, s32[1,7]{1,0:T(1,128)} %slot_hbm.1, s32[1,7]{1,0:T(1,128)} %start_hbm.1), custom_call_target="tpu_custom_call" | custom-call | tf_op jit(solution)/shard_map/pallas_call | solution.py:236
  43.2 0.7 %copy.7 = f32[128,512]{1,0:T(8,128)} copy(f32[128,512]{1,0:T(8,128)S(1)} %shard_map.55) | data formatting | bytes 524288

commit v3 on v2

--- a/solution.py
+++ b/solution.py
@@ -11,7 +11,12 @@
 NTAB = 4
 RANGE = 3
 REACH = 2 * RANGE + 1
-SIZES = (16, 16, 32, 32, 32)
+SIZES = (16,) * 8
+HEAD = 32
+PLANE = 32
+STEP = 24
+DIRECT = 5
+LAG = 1
 CHUNKS = len(SIZES)
 LANES = 128
 MESH = pl.DeviceIdType.MESH
@@ -20,9 +25,10 @@
 
 def kernel(
     n_slab, traces_ref, tables_ref, span_hbm, slot_hbm, start_hbm, out_ref,
-    span_ref, slot_ref, start_ref, trace_v, moves, win, got, slots_out, slots_in,
-    stack, sums, land, tab,
+    span_ref, slot_ref, start_ref, trace_a, trace_b, moves, win, got, slots_out, slots_in,
+    stack, sums, land, tab, held,
     int_sem, load_sem, tab_sem, slot_send, slot_recv, win_send, win_recv, z_send, z_recv, hello,
+    held_send, held_recv,
 ):
     slab = lax.axis_index("slab")
     det = lax.axis_index("det")
@@ -34,7 +40,7 @@
     second = (across, side)
     keeps = (keep_a, keep_b)
     gives = (1 - keep_a, 5 - keep_b)
-    n_tiles = trace_v.shape[0]
+    n_tiles = trace_a.shape[0]
     near = jnp.minimum(slab, RANGE) + jnp.minimum(n_slab - 1 - slab, RANGE)
 
     def inside(s):
@@ -42,6 +48,30 @@
 
     def piece(c):
         return pl.ds(sum(SIZES[:c]), SIZES[c])
+
+    def leaves(s, o):
+        return jnp.logical_and(inside(s + o), (s + o + PLANE) // PLANE != (s + PLANE) // PLANE)
+
+    def aid(target, way):
+        return target + way * STEP
+
+    ways = (-1, 1)
+    served = [slab - way * STEP for way in ways]
+    passes = [
+        [
+            functools.reduce(
+                jnp.logical_and,
+                [
+                    inside(served[w]),
+                    (served[w] + PLANE) // PLANE == (slab + PLANE) // PLANE,
+                    leaves(served[w], -way * a),
+                ],
+            )
+            for a in range(1, RANGE + 1)
+        ]
+        for w, way in enumerate(ways)
+    ]
+    n_passes = [sum(p.astype(jnp.int32) for p in passes[w]) for w in range(2)]
 
     def wait_bytes(ref, sem):
         pltpu.make_async_copy(ref, ref, sem).wait()
@@ -57,6 +87,10 @@
     greets_side = jnp.logical_or(det == 0, det == 3)
     greets_across = det < 2
     friends = near + jnp.where(det == 2, 2, jnp.where(det == 0, 0, 1))
+    for w in range(2):
+        friends = friends + jnp.minimum(n_passes[w], 1)
+    for o in OFFSETS:
+        friends = friends + leaves(slab, o).astype(jnp.int32)
 
     @pl.when(greets_side)
     def _():
@@ -71,6 +105,22 @@
         @pl.when(inside(slab + o))
         def _():
             pl.semaphore_signal(barrier, inc=1, device_id=(slab + o, det), device_id_type=MESH)
+
+    for w, way in enumerate(ways):
+
+        @pl.when(leaves(slab, -way * RANGE))
+        def _():
+            pl.semaphore_signal(
+                barrier, inc=1, device_id=(aid(slab, way), det), device_id_type=MESH
+            )
+
+        for a in range(1, RANGE + 1):
+
+            @pl.when(passes[w][a - 1])
+            def _():
+                pl.semaphore_signal(
+                    barrier, inc=1, device_id=(served[w] - way * a, det), device_id_type=MESH
+                )
 
     ints = [
         pltpu.make_async_copy(src, dst, int_sem.at[n])
@@ -81,12 +131,17 @@
     for copy in ints:
         copy.start()
 
-    @pl.loop(0, n_tiles)
-    def _(tile):
-        pltpu.make_async_copy(
-            traces_ref.at[0, :, pl.ds(pl.multiple_of(tile * LANES, LANES), LANES)],
-            trace_v.at[tile], load_sem,
-        ).start()
+    for part, (buffer, top) in enumerate([(trace_a, 0), (trace_b, HEAD)]):
+
+        @pl.loop(0, n_tiles)
+        def _(tile):
+            pltpu.make_async_copy(
+                traces_ref.at[
+                    0, pl.ds(top, buffer.shape[1]),
+                    pl.ds(pl.multiple_of(tile * LANES, LANES), LANES),
+                ],
+                buffer.at[tile], load_sem.at[part],
+            ).start()
 
     tab_load = pltpu.make_async_copy(tables_ref, tab, tab_sem)
 
@@ -116,7 +171,12 @@
     def cut(q, o, c):
         tile = lax.div(start_ref[0, o + RANGE], LANES)
         last = lax.min(tile + 2, n_tiles - 1)
-        tiles = [trace_v[spot, piece(c), :].astype(jnp.bfloat16) for spot in (tile, tile + 1, last)]
+        top = sum(SIZES[:c])
+        buffer, top = (trace_a, top) if top < HEAD else (trace_b, top - HEAD)
+        tiles = [
+            buffer[spot, pl.ds(top, SIZES[c]), :].astype(jnp.bfloat16)
+            for spot in (tile, tile + 1, last)
+        ]
         for h in range(2):
             pair = jnp.concatenate([tiles[h], tiles[h + 1]], axis=1)
             win[q, piece(c), pl.ds(h * LANES, LANES)] = jnp.dot(
@@ -141,9 +201,12 @@
     def wait_step(step, c):
         wait_bytes(land.at[step, :, piece(c), :], z_recv.at[step, c])
 
-    wait_bytes(trace_v, load_sem)
-    tab_load.start()
     for c in range(CHUNKS):
+        if c == 0:
+            wait_bytes(trace_a, load_sem.at[0])
+        if sum(SIZES[:c]) == HEAD:
+            wait_bytes(trace_b, load_sem.at[1])
+            tab_load.start()
         for q, o in enumerate([*OFFSETS, 0]):
             cut(q, o, c)
         if c == 0:
@@ -163,7 +226,18 @@
 
         for q, o in enumerate(OFFSETS):
 
-            @pl.when(inside(slab + o))
+            far = leaves(slab, o) if c >= DIRECT else False
+            if c >= DIRECT:
+                w, way = (0, -1) if o < 0 else (1, 1)
+
+                @pl.when(far)
+                def _():
+                    send(
+                        win.at[q, piece(c), :], held.at[w, abs(o) - 1, piece(c), :],
+                        win_send, held_recv.at[w, c - DIRECT], (aid(slab + o, way), det),
+                    )
+
+            @pl.when(jnp.logical_and(inside(slab + o), jnp.logical_not(far)))
             def _():
                 if c == 0:
                     send(slots_out.at[q], slots_in.at[q], slot_send, slot_recv, (slab + o, det))
@@ -171,6 +245,24 @@
                     win.at[q, piece(c), :], got.at[q, piece(c), :],
                     win_send, win_recv.at[c], (slab + o, det),
                 )
+
+    def pass_on(c):
+        for w, way in enumerate(ways):
+            for n in range(1, RANGE + 1):
+
+                @pl.when(n_passes[w] == n)
+                def _():
+                    wait_bytes(held.at[w, pl.ds(0, n), piece(c), :], held_recv.at[w, c - DIRECT])
+
+            for a in range(1, RANGE + 1):
+
+                @pl.when(passes[w][a - 1])
+                def _():
+                    send(
+                        held.at[w, a - 1, piece(c), :],
+                        got.at[OFFSETS.index(way * a), piece(c), :],
+                        held_send, win_recv.at[c], (served[w], det),
+                    )
 
     wait_near(lambda n: slots_in.at[pl.ds(0, n)], slot_recv)
     for c in range(CHUNKS):
@@ -198,6 +290,9 @@
                 pl.semaphore_wait(hello.at[1], 1)
 
         send_step(0, c)
+        for late in range(DIRECT, CHUNKS):
+            if c == min(late + LAG, CHUNKS - 1):
+                pass_on(late)
 
     for step in range(2):
         for c in range(CHUNKS):
@@ -226,6 +321,13 @@
     wait_near(lambda n: slots_out.at[pl.ds(0, n)], slot_send)
     wait_near(lambda n: win.at[pl.ds(0, n)], win_send)
     wait_bytes(land, z_send)
+    for w in range(2):
+        for n in range(1, RANGE + 1):
+
+            @pl.when(n_passes[w] == n)
+            def _():
+                passed = pl.ds(sum(SIZES[:DIRECT]), sum(SIZES[DIRECT:]))
+                wait_bytes(held.at[w, pl.ds(0, n), passed, :], held_send)
 
 
 def body(n_slab, traces, tables, slab_range, table_slot, sample_start):
@@ -242,7 +344,8 @@
             pltpu.SMEM((1, 2), jnp.int32),
             pltpu.SMEM((1, REACH), jnp.int32),
             pltpu.SMEM((1, REACH), jnp.int32),
-            pltpu.VMEM((samp // LANES, frames, LANES), jnp.float32),
+            pltpu.VMEM((samp // LANES, HEAD, LANES), jnp.float32),
+            pltpu.VMEM((samp // LANES, frames - HEAD, LANES), jnp.float32),
             pltpu.VMEM((REACH, 2 * LANES, LANES), jnp.bfloat16),
             pltpu.VMEM((REACH, frames, KWIN), jnp.bfloat16),
             pltpu.VMEM((2 * RANGE, frames, KWIN), jnp.bfloat16),
@@ -252,8 +355,10 @@
             pltpu.VMEM((2, 2, frames, KWIN), jnp.bfloat16),
             pltpu.VMEM((3, 2, frames, KWIN), jnp.bfloat16),
             pltpu.VMEM((NTAB, KWIN, vox), jnp.bfloat16),
-            dma((3,)), dma, dma, dma, dma, dma, dma((CHUNKS,)), dma, dma((3, CHUNKS)),
+            pltpu.VMEM((2, RANGE, frames, KWIN), jnp.bfloat16),
+            dma((3,)), dma((2,)), dma, dma, dma, dma, dma((CHUNKS,)), dma, dma((3, CHUNKS)),
             pltpu.SemaphoreType.REGULAR((2,)),
+            dma, dma((2, CHUNKS - DIRECT)),
         ],
         compiler_params=pltpu.CompilerParams(collective_id=0, has_side_effects=True),
     )(traces, tables, slab_range, table_slot, sample_start)

time: 44.1 us -> 41.9 us (0.950)
  Pallas kernels: 43.2 us -> 41 us
    pallas_call x1, Pallas kernels: 43.2 us -> 41 us  [body(): pl.pallas_call(functools.partial(kernel, n_slab), out_shape=pltpu.VMEM((f...]
where the time goes in v3:
time: 41.9 us; the launch traced here: 41.7 us
  Pallas kernels  41 us (98%)
  local copies, waits for them, and re-layouts  0.71 us (2%)
    pallas_call x1, Pallas kernels, body(): pl.pallas_call(functools.partial(kernel, n_slab), out_shape=pltpu.VMEM((f...  41 us

profile of v3, /device:TPU:30, one launch (start us, length us, event | category | flops | bytes accessed | tf_op | source)
XLA Modules:
  0.0 41.7 jit_solution(5138261734603062757)
XLA Ops:
  0.0 41.0 %shard_map.55 = f32[128,512]{1,0:T(8,128)S(1)} custom-call(f32[1,128,4096]{2,1,0:T(8,128)} %traces_ref.1, bf16[4,256,512]{2,1,0:T(8,128)(2,1)} %tables_ref.1, s32[1,2]{1,0:T(1,128)} %span_hbm.1, s32[1,7]{1,0:T(1,128)} %slot_hbm.1, s32[1,7]{1,0:T(1,128)} %start_hbm.1), custom_call_target="tpu_custom_call" | custom-call | tf_op jit(solution)/shard_map/pallas_call | solution.py:338
  41.0 0.7 %copy.7 = f32[128,512]{1,0:T(8,128)} copy(f32[128,512]{1,0:T(8,128)S(1)} %shard_map.55) | data formatting | bytes 524288

commit v4 on v3

--- a/solution.py
+++ b/solution.py
@@ -16,9 +16,10 @@
 PLANE = 32
 STEP = 24
 DIRECT = 5
-LAG = 1
+LAG = 0
 CHUNKS = len(SIZES)
 LANES = 128
+SUB = 8
 MESH = pl.DeviceIdType.MESH
 OFFSETS = [3, -3, 2, -2, 1, -1]
 
@@ -40,7 +41,7 @@
     second = (across, side)
     keeps = (keep_a, keep_b)
     gives = (1 - keep_a, 5 - keep_b)
-    n_tiles = trace_a.shape[0]
+    n_tiles = trace_a.shape[1]
     near = jnp.minimum(slab, RANGE) + jnp.minimum(n_slab - 1 - slab, RANGE)
 
     def inside(s):
@@ -131,18 +132,14 @@
     for copy in ints:
         copy.start()
 
-    for part, (buffer, top) in enumerate([(trace_a, 0), (trace_b, HEAD)]):
-
-        @pl.loop(0, n_tiles)
-        def _(tile):
-            pltpu.make_async_copy(
-                traces_ref.at[
-                    0, pl.ds(top, buffer.shape[1]),
-                    pl.ds(pl.multiple_of(tile * LANES, LANES), LANES),
-                ],
-                buffer.at[tile], load_sem.at[part],
-            ).start()
-
+    loads = [
+        pltpu.make_async_copy(
+            traces_ref.at[pl.ds(top // SUB, buffer.shape[0])], buffer, load_sem.at[part]
+        )
+        for part, (buffer, top) in enumerate([(trace_a, 0), (trace_b, HEAD)])
+    ]
+    for load in loads:
+        load.start()
     tab_load = pltpu.make_async_copy(tables_ref, tab, tab_sem)
 
     for copy in ints:
@@ -174,7 +171,9 @@
         top = sum(SIZES[:c])
         buffer, top = (trace_a, top) if top < HEAD else (trace_b, top - HEAD)
         tiles = [
-            buffer[spot, pl.ds(top, SIZES[c]), :].astype(jnp.bfloat16)
+            buffer[pl.ds(top // SUB, SIZES[c] // SUB), spot]
+            .reshape(SIZES[c], LANES)
+            .astype(jnp.bfloat16)
             for spot in (tile, tile + 1, last)
         ]
         for h in range(2):
@@ -203,9 +202,9 @@
 
     for c in range(CHUNKS):
         if c == 0:
-            wait_bytes(trace_a, load_sem.at[0])
+            loads[0].wait()
         if sum(SIZES[:c]) == HEAD:
-            wait_bytes(trace_b, load_sem.at[1])
+            loads[1].wait()
             tab_load.start()
         for q, o in enumerate([*OFFSETS, 0]):
             cut(q, o, c)
@@ -333,6 +332,7 @@
 def body(n_slab, traces, tables, slab_range, table_slot, sample_start):
     _, frames, samp = traces.shape
     vox = tables.shape[2]
+    traces = traces.reshape(frames // SUB, SUB, samp // LANES, LANES).transpose(0, 2, 1, 3)
     far = pl.BlockSpec(memory_space=pl.ANY)
     dma = pltpu.SemaphoreType.DMA
     return pl.pallas_call(
@@ -344,8 +344,8 @@
             pltpu.SMEM((1, 2), jnp.int32),
             pltpu.SMEM((1, REACH), jnp.int32),
             pltpu.SMEM((1, REACH), jnp.int32),
-            pltpu.VMEM((samp // LANES, HEAD, LANES), jnp.float32),
-            pltpu.VMEM((samp // LANES, frames - HEAD, LANES), jnp.float32),
+            pltpu.VMEM((HEAD // SUB, samp // LANES, SUB, LANES), jnp.float32),
+            pltpu.VMEM(((frames - HEAD) // SUB, samp // LANES, SUB, LANES), jnp.float32),
             pltpu.VMEM((REACH, 2 * LANES, LANES), jnp.bfloat16),
             pltpu.VMEM((REACH, frames, KWIN), jnp.bfloat16),
             pltpu.VMEM((2 * RANGE, frames, KWIN), jnp.bfloat16),

time: 41.9 us -> 41.8 us (level)
  no operation moved by 1% of the time
where the time goes in v4:
time: 41.8 us; the launch traced here: 41.7 us
  Pallas kernels  41 us (98%)
  local copies, waits for them, and re-layouts  0.71 us (2%)
    pallas_call x1, Pallas kernels, body(): pl.pallas_call(functools.partial(kernel, n_slab), out_shape=pltpu.VMEM((f...  41 us

profile of v4, /device:TPU:30, one launch (start us, length us, event | category | flops | bytes accessed | tf_op | source)
XLA Modules:
  0.0 41.7 jit_solution(18162332850268922122)
XLA Ops:
  0.0 41.0 %shard_map.55 = f32[128,512]{1,0:T(8,128)S(1)} custom-call(f32[16,32,8,128]{3,2,1,0:T(8,128)} %bitcast.3, bf16[4,256,512]{2,1,0:T(8,128)(2,1)} %tables_ref.1, s32[1,2]{1,0:T(1,128)} %span_hbm.1, s32[1,7]{1,0:T(1,128)} %slot_hbm.1, s32[1,7]{1,0:T(1,128)} %start_hbm.1), custom_call_target="tpu_custom_call" | custom-call | tf_op jit(solution)/shard_map/pallas_call | solution.py:338
  41.0 0.7 %copy.7 = f32[128,512]{1,0:T(8,128)} copy(f32[128,512]{1,0:T(8,128)S(1)} %shard_map.55) | data formatting | bytes 524288

commit v5 on v4

--- a/solution.py
+++ b/solution.py
@@ -28,7 +28,7 @@
     n_slab, traces_ref, tables_ref, span_hbm, slot_hbm, start_hbm, out_ref,
     span_ref, slot_ref, start_ref, trace_a, trace_b, moves, win, got, slots_out, slots_in,
     stack, sums, land, tab, held,
-    int_sem, load_sem, tab_sem, slot_send, slot_recv, win_send, win_recv, z_send, z_recv, hello,
+    int_sem, load_sem, tab_sem, slot_send, slot_recv, win_send, win_recv, z_send, z_recv, z_last, hello,
     held_send, held_recv,
 ):
     slab = lax.axis_index("slab")
@@ -193,7 +193,7 @@
             src = stack.at[gives[cls]] if step == 0 else sums.at[step - 1, cls]
             send(
                 src.at[piece(c), :], land.at[step, cls, piece(c), :],
-                z_send, z_recv.at[step, c],
+                z_send, z_last.at[c // 2] if step == 2 else z_recv.at[step, c],
                 (slab, (second if step == 1 else first)[cls]),
             )
 
@@ -308,14 +308,15 @@
     out_ref[...] = jnp.dot(
         sums[1, 0], tab[keeps[0]], preferred_element_type=jnp.float32
     ) + jnp.dot(sums[1, 1], tab[keeps[1]], preferred_element_type=jnp.float32)
-    for c in range(CHUNKS):
-        wait_step(2, c)
-        total = out_ref[piece(c), :]
+    for pair in range(CHUNKS // 2):
+        both = pl.ds(sum(SIZES[: 2 * pair]), SIZES[2 * pair] + SIZES[2 * pair + 1])
+        wait_bytes(land.at[2, :, both, :], z_last.at[pair])
+        total = out_ref[both, :]
         for cls in range(2):
             total = total + jnp.dot(
-                land[2, cls, piece(c), :], tab[gives[cls]], preferred_element_type=jnp.float32
+                land[2, cls, both, :], tab[gives[cls]], preferred_element_type=jnp.float32
             )
-        out_ref[piece(c), :] = total
+        out_ref[both, :] = total
 
     wait_near(lambda n: slots_out.at[pl.ds(0, n)], slot_send)
     wait_near(lambda n: win.at[pl.ds(0, n)], win_send)
@@ -356,7 +357,7 @@
             pltpu.VMEM((3, 2, frames, KWIN), jnp.bfloat16),
             pltpu.VMEM((NTAB, KWIN, vox), jnp.bfloat16),
             pltpu.VMEM((2, RANGE, frames, KWIN), jnp.bfloat16),
-            dma((3,)), dma((2,)), dma, dma, dma, dma, dma((CHUNKS,)), dma, dma((3, CHUNKS)),
+            dma((3,)), dma((2,)), dma, dma, dma, dma, dma((CHUNKS,)), dma, dma((2, CHUNKS)), dma((CHUNKS // 2,)),
             pltpu.SemaphoreType.REGULAR((2,)),
             dma, dma((2, CHUNKS - DIRECT)),
         ],

time: 41.8 us -> 41.7 us (level)
  the two profiles are of different devices: /device:TPU:30 before, /device:TPU:62 now
where the time goes in v5:
time: 41.7 us; the launch traced here: 41.6 us
  Pallas kernels  40.8 us (98%)
  local copies, waits for them, and re-layouts  0.71 us (2%)
    pallas_call x1, Pallas kernels, body(): pl.pallas_call(functools.partial(kernel, n_slab), out_shape=pltpu.VMEM((f...  40.8 us

profile of v5, /device:TPU:62, one launch (start us, length us, event | category | flops | bytes accessed | tf_op | source)
XLA Modules:
  0.0 41.6 jit_solution(12008329214909954234)
XLA Ops:
  0.0 40.8 %shard_map.55 = f32[128,512]{1,0:T(8,128)S(1)} custom-call(f32[16,32,8,128]{3,2,1,0:T(8,128)} %bitcast.3, bf16[4,256,512]{2,1,0:T(8,128)(2,1)} %tables_ref.1, s32[1,2]{1,0:T(1,128)} %span_hbm.1, s32[1,7]{1,0:T(1,128)} %slot_hbm.1, s32[1,7]{1,0:T(1,128)} %start_hbm.1), custom_call_target="tpu_custom_call" | custom-call | tf_op jit(solution)/shard_map/pallas_call | solution.py:339
  40.9 0.7 %copy.7 = f32[128,512]{1,0:T(8,128)} copy(f32[128,512]{1,0:T(8,128)S(1)} %shard_map.55) | data formatting | bytes 524288
